TPU v7x, 128 devices: a whole 4x4x4 slice. The times are simulated.
128 devices in a mesh: row: 2 (over z_lo), col: 64 (over y, x, z_hi, core).
Axes of the slice: x: 4, y: 4, z: 4 (z_hi: 2, z_lo: 2; z = z_hi * 2 + z_lo), core: 2. Of those that a mesh axis runs over, the one named last changes fastest.
Arguments:
- tokens: bfloat16 [512, 4608], P('col', 'row'), may hold values from -6 to 6
- pre_gain: float32 [2, 4608], P(None, 'row'), may hold values from -0.6 to 0.6
- post_gain: float32 [2, 4608], P(None, 'row'), may hold values from -0.6 to 0.6
- gate_weight: bfloat16 [2, 4608, 36864], P(None, ('row', 'col')), may hold values from -0.09375 to 0.09375
- up_weight: bfloat16 [2, 4608, 36864], P(None, ('row', 'col')), may hold values from -0.09375 to 0.09375
- down_weight: bfloat16 [2, 36864, 4608], P(None, ('row', 'col')), may hold values from -0.13541667 to 0.13541667
Outputs:
- stream: bfloat16 [512, 4608], P('col', 'row')
All inputs are finite; a program needn't handle non-finite values.
Results may differ from a plain program's by a relative error of at most 0.019.
Values may be sent and summed in bfloat16 or wider, within the bound.
A program may use at most 128 MiB of HBM per device.

v0:
```python
import jax
import jax.numpy as jnp
from jax import lax
from jax.sharding import Mesh
from jax.sharding import PartitionSpec as P

COL = ("col_0", "col_1", "col_2", "col_3")
ROW_COL = ("row", "col_0", "col_1", "col_2", "col_3")
norm_eps = 1e-06


def sent_to_all(value, axis):
    copies = jnp.broadcast_to(value, (lax.axis_size(axis), *value.shape))
    return lax.all_to_all(copies, axis, split_axis=0, concat_axis=0, tiled=True)


def over_copies(value, axis):
    everything = sent_to_all(value, axis)
    return jnp.sum(everything, axis=0)


def laid_out(blocks, dim):
    lengths = list(blocks.shape[1:])
    lengths[dim] *= blocks.shape[0]
    return jnp.moveaxis(blocks, 0, dim).reshape(lengths)


def whole_of(value, axes, dim):
    far, near = axes
    first = sent_to_all(value, far)
    blocks = jnp.swapaxes(sent_to_all(first, near), 0, 1)
    return laid_out(blocks.reshape(-1, *value.shape), dim)


def over_copies_2(value, axis):
    everything = sent_to_all(value, axis)
    return jnp.sum(everything.astype(jnp.float32), axis=0)


def split_up(value, dim, peers):
    before, after = (value.shape[:dim], value.shape[dim + 1 :])
    return jnp.moveaxis(value.reshape(*before, peers, -1, *after), dim, 0)


def summed_on_arrival(value, axis, dim):
    peers = lax.axis_size(axis)
    blocks = lax.all_to_all(split_up(value, dim, peers), axis, 0, 0, tiled=True)
    return jnp.sum(blocks.astype(jnp.float32), axis=0)


def sum_by_axis(value, axes, dim):
    far, near = axes
    blocks = split_up(value, dim, lax.axis_size(far))
    nearer = summed_on_arrival(blocks, near, dim + 1)
    arrived = lax.all_to_all(
        nearer.astype(jnp.bfloat16), far, split_axis=0, concat_axis=0, tiled=True
    )
    return arrived.astype(jnp.float32).sum(axis=0)


def activate(summed, columns):
    gate = summed[:, :columns]
    up_proj = summed[:, columns:]
    return (jax.nn.gelu(gate, approximate=True) * up_proj).astype(jnp.bfloat16)


def on_device(tokens, pre_gain, post_gain, gate_weight, up_weight, down_weight):
    layer_count = gate_weight.shape[0]
    row_count = lax.axis_size("row")
    col_count = lax.axis_size(COL)
    model_width = tokens.shape[1] * row_count
    stored_rows = gate_weight.shape[1]
    hidden_total = gate_weight.shape[2]
    block_width = hidden_total // (row_count * col_count)
    tile_rows = stored_rows * col_count
    tile_columns = hidden_total // col_count
    gate_split = gate_weight.reshape(layer_count, stored_rows, row_count, col_count, block_width)
    up_split = up_weight.reshape(layer_count, stored_rows, row_count, col_count, block_width)
    gate_tiles, up_tiles = (
        lax.all_to_all(gate_split, COL, split_axis=3, concat_axis=1, tiled=True),
        lax.all_to_all(up_split, COL, split_axis=3, concat_axis=1, tiled=True),
    )
    gate_tiles = gate_tiles.reshape(layer_count, tile_rows, tile_columns)
    up_tiles = up_tiles.reshape(layer_count, tile_rows, tile_columns)
    down_tiles = lax.all_to_all(down_weight, "row", split_axis=2, concat_axis=1, tiled=True)
    current = tokens
    for layer_index in range(layer_count):
        gate_up = jnp.concatenate((gate_tiles[layer_index], up_tiles[layer_index]), axis=1)
        down_tile = down_tiles[layer_index]
        columns = gate_up.shape[1] // 2
        values = current.astype(jnp.float32)
        squares = over_copies(jnp.sum(values * values, axis=1), "row")
        scale_pre = lax.rsqrt(squares / model_width + norm_eps)[:, None]
        normed = (values * scale_pre * (1.0 + pre_gain[layer_index])[None, :]).astype(jnp.bfloat16)
        partial_sums = jnp.dot(
            whole_of(normed, (("col_0", "col_1", "col_2"), "col_3"), 0),
            gate_up,
            preferred_element_type=jnp.float32,
        )
        summed = over_copies_2(partial_sums.astype(jnp.bfloat16), "row").astype(jnp.float32)
        hidden = activate(summed, columns)
        branch = sum_by_axis(
            jnp.dot(hidden, down_tile, preferred_element_type=jnp.float32).astype(jnp.bfloat16),
            (("col_0", "col_1", "col_2"), "col_3"),
            0,
        )
        branch_squares = over_copies(jnp.sum(branch * branch, axis=1), "row")
        scale_post = lax.rsqrt(branch_squares / model_width + norm_eps)[:, None]
        post = branch * scale_post * (1.0 + post_gain[layer_index])[None, :]
        current = (values + post).astype(jnp.bfloat16)
    return current


def solution(mesh):
    split = Mesh(
        mesh.devices.reshape(mesh.shape["row"], 4, 4, 2, 2),
        ("row", "col_0", "col_1", "col_2", "col_3"),
    )
    in_specs = (
        P(COL, "row"),
        P(None, "row"),
        P(None, "row"),
        P(None, ROW_COL, None),
        P(None, ROW_COL, None),
        P(None, ROW_COL, None),
    )
    out_specs = P(COL, "row")
    return jax.shard_map(
        on_device, mesh=split, in_specs=in_specs, out_specs=out_specs, check_vma=False
    )
```

profile of v0, /device:TPU:0, one launch (start us, length us, event | category | flops | bytes accessed | tf_op | source)
XLA Modules:
  0.0 576.6 jit_solution(1357578688195838266)
XLA Ops:
  0.0 0.9 fusion.42
  1.5 3.3 all-to-all-start
  4.8 1.4 add_reduce_fusion.1
  6.2 2.3 all-to-all-done
  8.5 0.8 fusion.44
  9.3 1.1 broadcast_in_dim.39
  10.5 10.6 %all-to-all-start.1 = ((bf16[32,8,2304]{2,1,0:T(8,128)(2,1)}), bf16[32,8,2304]{2,1,0:T(8,128)(2,1)S(1)}, u32[]{:S(2)}, u32[]{:S(2)}) async-start(bf16[32,8,2304]{2,1,0:T(8,128)(2,1)} %broadcast_in_dim.39), calls=%async_computation.1 | async-start | bytes 2359296 | tf_op jit(solution)/shard_map/all_to_all | solution.py:14
  21.1 14.4 %reshape.58 = bf16[2,36,2,64,288]{4,3,2,0,1:T(8,128)(2,1)} reshape(bf16[2,36,36864]{2,0,1:T(2,128)(2,1)} %param.9) | data formatting | bytes 10616832 | tf_op jit(solution)/shard_map/reshape | solution.py:77
  35.5 11.5 %copy.43 = bf16[2,36,2,64,288]{4,2,1,0,3:T(2,128)(2,1)} copy(bf16[2,36,2,64,288]{4,3,2,0,1:T(8,128)(2,1)} %reshape.58) | data formatting | bytes 10616832 | tf_op jit(solution)/shard_map/reshape | solution.py:77
  47.1 5.6 all_to_all.119
  52.7 10.6 %all-to-all-start.3 = ((bf16[2,36,2,64,288]{4,2,1,0,3:T(2,128)(2,1)}), bf16[2,36,2,64,288]{4,2,1,0,3:T(2,128)(2,1)}, u32[]{:S(2)}, u32[]{:S(2)}) async-start(bf16[2,36,2,64,288]{4,2,1,0,3:T(2,128)(2,1)} %copy.43), calls=%async_computation.3 | async-start | bytes 14155776 | tf_op jit(solution)/shard_map/all_to_all | solution.py:80
  63.4 14.4 %reshape.59 = bf16[2,36,2,64,288]{4,3,2,0,1:T(8,128)(2,1)} reshape(bf16[2,36,36864]{2,0,1:T(2,128)(2,1)} %param.10) | data formatting | bytes 10616832 | tf_op jit(solution)/shard_map/reshape | solution.py:78
  77.8 11.5 %copy.44 = bf16[2,36,2,64,288]{4,2,1,0,3:T(2,128)(2,1)} copy(bf16[2,36,2,64,288]{4,3,2,0,1:T(8,128)(2,1)} %reshape.59) | data formatting | bytes 10616832 | tf_op jit(solution)/shard_map/reshape | solution.py:78
  89.3 62.8 %all-to-all-done.3 = bf16[2,36,2,64,288]{4,2,1,0,3:T(2,128)(2,1)} async-done(((bf16[2,36,2,64,288]{4,2,1,0,3:T(2,128)(2,1)}), bf16[2,36,2,64,288]{4,2,1,0,3:T(2,128)(2,1)}, u32[]{:S(2)}, u32[]{:S(2)}) %all-to-all-start.3) | async-done | bytes 5308448 | tf_op jit(solution)/shard_map/all_to_all | solution.py:80
  152.1 16.1 %all-to-all-start.4 = ((bf16[2,36,2,64,288]{4,2,1,0,3:T(2,128)(2,1)}), bf16[2,36,2,64,288]{4,2,1,0,3:T(2,128)(2,1)}, u32[]{:S(2)}, u32[]{:S(2)}) async-start(bf16[2,36,2,64,288]{4,2,1,0,3:T(2,128)(2,1)} %copy.44), calls=%async_computation.4 | async-start | bytes 14155776 | tf_op jit(solution)/shard_map/all_to_all | solution.py:81
  168.1 18.0 %copy.45 = bf16[2,288,4608]{1,0,2:T(2,128)(2,1)} copy(bf16[2,288,4608]{2,1,0:T(8,128)(2,1)} %param.11) | data formatting | bytes 10616832 | tf_op args[5]
  186.1 1.6 copy.42
  187.7 69.1 %all-to-all-done.4 = bf16[2,36,2,64,288]{4,2,1,0,3:T(2,128)(2,1)} async-done(((bf16[2,36,2,64,288]{4,2,1,0,3:T(2,128)(2,1)}), bf16[2,36,2,64,288]{4,2,1,0,3:T(2,128)(2,1)}, u32[]{:S(2)}, u32[]{:S(2)}) %all-to-all-start.4) | async-done | bytes 5308448 | tf_op jit(solution)/shard_map/all_to_all | solution.py:81
  256.8 6.8 %all-to-all-start.6 = ((bf16[2,288,4608]{1,0,2:T(2,128)(2,1)}), bf16[2,288,4608]{1,0,2:T(2,128)(2,1)}, u32[]{:S(2)}, u32[]{:S(2)}) async-start(bf16[2,288,4608]{1,0,2:T(2,128)(2,1)} %copy.45), calls=%async_computation.6 | async-start | bytes 14155776 | tf_op jit(solution)/shard_map/all_to_all | solution.py:85
  263.7 9.8 %fusion.61 = (bf16[1,64,36,2,1,288]{5,3,2,0,1,4:T(2,128)(2,1)S(1)}, bf16[1,64,36,2,1,288]{5,3,2,0,1,4:T(2,128)(2,1)}) fusion(bf16[2,64,36,2,1,288]{5,3,2,0,1,4:T(2,128)(2,1)} %bitcast.4), kind=kLoop, calls=%fused_computation.80 | loop fusion | bytes 10616832 | tf_op jit(solution)/shard_map/slice | solution.py:88
  273.5 8.5 %squeeze.22 = bf16[2304,576]{1,0:T(8,128)(2,1)} reshape(bf16[1,64,36,2,1,288]{5,3,2,0,1,4:T(2,128)(2,1)} %get-tuple-element.12) | data formatting | bytes 5308416 | tf_op jit(solution)/shard_map/squeeze | solution.py:88
  282.0 10.8 %fusion.62 = (bf16[1,64,36,2,1,288]{5,3,2,0,1,4:T(2,128)(2,1)}, bf16[1,64,36,2,1,288]{5,3,2,0,1,4:T(2,128)(2,1)}) fusion(bf16[2,64,36,2,1,288]{5,3,2,0,1,4:T(2,128)(2,1)} %bitcast.6), kind=kLoop, calls=%fused_computation.81 | loop fusion | bytes 10616832 | tf_op jit(solution)/shard_map/slice | solution.py:88
  292.7 8.0 %squeeze.23 = bf16[2304,576]{1,0:T(8,128)(2,1)} reshape(bf16[1,64,36,2,1,288]{5,3,2,0,1,4:T(2,128)(2,1)} %get-tuple-element.14) | data formatting | bytes 5308416 | tf_op jit(solution)/shard_map/squeeze | solution.py:88
  300.7 7.7 %fusion.11 = bf16[512,1152]{1,0:T(8,128)(2,1)} fusion(bf16[512,2304]{1,0:T(8,128)(2,1)} %bitcast.49, bf16[2304,576]{1,0:T(8,128)(2,1)} %squeeze.23, bf16[2304,576]{1,0:T(8,128)(2,1)} %squeeze.22), kind=kOutput, calls=%fused_computation.13 | convolution fusion | flops 2729115648 | bytes 8847360 | tf_op jit(solution)/shard_map/dot_general | solution.py:95
  308.4 33.6 %all-to-all-done.6 = bf16[2,288,4608]{1,0,2:T(2,128)(2,1)} async-done(((bf16[2,288,4608]{1,0,2:T(2,128)(2,1)}), bf16[2,288,4608]{1,0,2:T(2,128)(2,1)}, u32[]{:S(2)}, u32[]{:S(2)}) %all-to-all-start.6) | async-done | bytes 5308448 | tf_op jit(solution)/shard_map/all_to_all | solution.py:85
  342.0 2.8 broadcast_in_dim.41
  344.8 4.9 all-to-all-start.5
  349.8 33.0 %copy.55 = bf16[2,288,2,2304]{3,2,1,0:T(2,128)(2,1)} copy(bf16[2,288,2,2304]{1,0,3,2:T(2,128)(2,1)} %bitcast.7) | data formatting | bytes 10616832 | tf_op jit(solution)/shard_map/all_to_all | solution.py:85
  382.8 7.0 %fusion.63 = (bf16[1,2,288,2304]{3,1,2,0:T(2,128)(2,1)}, bf16[1,2,288,2304]{3,1,2,0:T(2,128)(2,1)S(1)}) fusion(bf16[2,2,288,2304]{3,1,2,0:T(2,128)(2,1)} %bitcast.44), kind=kLoop, calls=%fused_computation.82 | loop fusion | bytes 10616832 | tf_op jit(solution)/shard_map/slice | solution.py:89
  389.8 1.8 copy.47
  391.6 2.5 convert_reduce_fusion.1
  394.1 2.3 convolution_convert_fusion.1
  396.6 6.5 %all_to_all.120 = bf16[2,32,8,2304]{3,2,1,0:T(8,128)(2,1)} all-to-all(bf16[2,32,8,2304]{3,2,1,0:T(8,128)(2,1)S(1)} %bitcast.45), channel_id=1, replica_groups=mesh['row'=2,'col_0'=4,'col_1'=4,'col_2'=2,'col_3'=2] {'col_3'}, dimensions={0} | all-to-all | bytes 4718592 | tf_op jit(solution)/shard_map/all_to_all | solution.py:47
  403.1 3.4 reduce_sum.135
  406.6 15.8 %all-to-all-start.8 = ((bf16[32,8,2304]{2,1,0:T(8,128)(2,1)}), bf16[32,8,2304]{2,1,0:T(8,128)(2,1)}, u32[]{:S(2)}, u32[]{:S(2)}) async-start(bf16[32,8,2304]{2,1,0:T(8,128)(2,1)} %reduce_sum.135), calls=%async_computation.8 | async-start | bytes 2359296 | tf_op jit(solution)/shard_map/all_to_all | solution.py:55
  422.4 1.5 add_reduce_fusion
  423.8 19.6 %all-to-all-done.8 = bf16[32,8,2304]{2,1,0:T(8,128)(2,1)} async-done(((bf16[32,8,2304]{2,1,0:T(8,128)(2,1)}), bf16[32,8,2304]{2,1,0:T(8,128)(2,1)}, u32[]{:S(2)}, u32[]{:S(2)}) %all-to-all-start.8) | async-done | bytes 1179680 | tf_op jit(solution)/shard_map/all_to_all | solution.py:55
  443.4 1.4 convert_reduce_fusion.3
  444.9 0.6 copy-done.4
  445.6 6.2 %all_to_all.121 = f32[2,1,8]{2,1,0:T(1,128)S(1)} all-to-all(f32[2,1,8]{2,1,0:T(1,128)S(1)} %broadcast_in_dim.42), channel_id=1, replica_groups=mesh['row'=2,'col_0'=4,'col_1'=4,'col_2'=2,'col_3'=2] {'row'}, dimensions={0} | all-to-all | bytes 128 | tf_op jit(solution)/shard_map/all_to_all | solution.py:14
  452.4 0.7 add_rsqrt_fusion.2
  453.0 1.7 fusion.46
  454.7 6.1 %all_to_all.122 = f32[2,1,8]{2,1,0:T(1,128)S(1)} all-to-all(f32[2,1,8]{2,1,0:T(1,128)S(1)} %broadcast_in_dim.43), channel_id=1, replica_groups=mesh['row'=2,'col_0'=4,'col_1'=4,'col_2'=2,'col_3'=2] {'row'}, dimensions={0} | all-to-all | bytes 128 | tf_op jit(solution)/shard_map/all_to_all | solution.py:14
  461.4 0.7 add_rsqrt_fusion.1
  462.1 0.9 fusion.48
  463.0 1.1 broadcast_in_dim.44
  464.0 4.7 all-to-all-start.11
  468.7 4.0 squeeze.25
  472.8 6.9 %squeeze.26 = bf16[2304,576]{1,0:T(8,128)(2,1)S(1)} reshape(bf16[1,64,36,2,1,288]{5,3,2,0,1,4:T(2,128)(2,1)} %get-tuple-element.13) | data formatting | bytes 5308416 | tf_op jit(solution)/shard_map/squeeze | solution.py:88
  479.7 6.5 %all-to-all-done.11 = bf16[32,8,2304]{2,1,0:T(8,128)(2,1)} async-done(((bf16[32,8,2304]{2,1,0:T(8,128)(2,1)}), bf16[32,8,2304]{2,1,0:T(8,128)(2,1)}, u32[]{:S(2)}, u32[]{:S(2)}) %all-to-all-start.11) | async-done | bytes 1179680 | tf_op jit(solution)/shard_map/all_to_all | solution.py:14
  486.2 1.4 broadcast_in_dim.45
  487.6 5.6 all_to_all.123
  493.4 1.7 copy-done.1
  495.1 3.2 fusion.8
  498.3 1.6 broadcast_in_dim.46
  500.0 5.4 all-to-all-start.13
  505.4 1.8 copy.52
  507.2 26.5 %all-to-all-done.13 = bf16[2,512,1152]{2,1,0:T(8,128)(2,1)} async-done(((bf16[2,512,1152]{2,1,0:T(8,128)(2,1)}), bf16[2,512,1152]{2,1,0:T(8,128)(2,1)}, u32[]{:S(2)}, u32[]{:S(2)}) %all-to-all-start.13) | async-done | bytes 2359328 | tf_op jit(solution)/shard_map/all_to_all | solution.py:14
  533.7 2.4 convert_reduce_fusion
  536.1 2.3 convolution_convert_fusion
  538.6 5.6 all_to_all.124
  544.8 24.4 %all_to_all.125 = bf16[32,8,2304]{2,1,0:T(8,128)(2,1)S(1)} all-to-all(bf16[32,8,2304]{2,1,0:T(8,128)(2,1)S(1)} %reduce_sum.142), channel_id=1, replica_groups=mesh['row'=2,'col_0'=4,'col_1'=4,'col_2'=2,'col_3'=2] {'col_0','col_1','..., dimensions={0} | all-to-all | bytes 2359296 | tf_op jit(solution)/shard_map/all_to_all | solution.py:55
  569.6 6.1 %all_to_all.126 = f32[2,1,8]{2,1,0:T(1,128)S(1)} all-to-all(f32[2,1,8]{2,1,0:T(1,128)S(1)} %broadcast_in_dim.47), channel_id=1, replica_groups=mesh['row'=2,'col_0'=4,'col_1'=4,'col_2'=2,'col_3'=2] {'row'}, dimensions={0} | all-to-all | bytes 128 | tf_op jit(solution)/shard_map/all_to_all | solution.py:14
  575.7 0.7 fusion.49
  (30 shorter events, 3.5 us)
Async XLA Ops:
  1.5 7.0 %all-to-all-start = ((f32[2,1,8]{2,1,0:T(1,128)}), f32[2,1,8]{2,1,0:T(1,128)S(1)}, u32[]{:S(2)}, u32[]{:S(2)}) async-start(f32[2,1,8]{2,1,0:T(1,128)} %broadcast_in_dim.38), calls=%async_computation | async-start | bytes 2048 | tf_op jit(solution)/shard_map/all_to_all | solution.py:14
  10.5 36.5 %all-to-all-start.1 = ((bf16[32,8,2304]{2,1,0:T(8,128)(2,1)}), bf16[32,8,2304]{2,1,0:T(8,128)(2,1)S(1)}, u32[]{:S(2)}, u32[]{:S(2)}) async-start(bf16[32,8,2304]{2,1,0:T(8,128)(2,1)} %broadcast_in_dim.39), calls=%async_computation.1 | async-start | bytes 2359296 | tf_op jit(solution)/shard_map/all_to_all | solution.py:14
  52.7 99.3 %all-to-all-start.3 = ((bf16[2,36,2,64,288]{4,2,1,0,3:T(2,128)(2,1)}), bf16[2,36,2,64,288]{4,2,1,0,3:T(2,128)(2,1)}, u32[]{:S(2)}, u32[]{:S(2)}) async-start(bf16[2,36,2,64,288]{4,2,1,0,3:T(2,128)(2,1)} %copy.43), calls=%async_computation.3 | async-start | bytes 14155776 | tf_op jit(solution)/shard_map/all_to_all | solution.py:80
  152.1 104.7 %all-to-all-start.4 = ((bf16[2,36,2,64,288]{4,2,1,0,3:T(2,128)(2,1)}), bf16[2,36,2,64,288]{4,2,1,0,3:T(2,128)(2,1)}, u32[]{:S(2)}, u32[]{:S(2)}) async-start(bf16[2,36,2,64,288]{4,2,1,0,3:T(2,128)(2,1)} %copy.44), calls=%async_computation.4 | async-start | bytes 14155776 | tf_op jit(solution)/shard_map/all_to_all | solution.py:81
  256.8 85.1 %all-to-all-start.6 = ((bf16[2,288,4608]{1,0,2:T(2,128)(2,1)}), bf16[2,288,4608]{1,0,2:T(2,128)(2,1)}, u32[]{:S(2)}, u32[]{:S(2)}) async-start(bf16[2,288,4608]{1,0,2:T(2,128)(2,1)} %copy.45), calls=%async_computation.6 | async-start | bytes 14155776 | tf_op jit(solution)/shard_map/all_to_all | solution.py:85
  344.8 46.8 %all-to-all-start.5 = ((bf16[2,512,1152]{2,1,0:T(8,128)(2,1)}), bf16[2,512,1152]{2,1,0:T(8,128)(2,1)}, u32[]{:S(2)}, u32[]{:S(2)}) async-start(bf16[2,512,1152]{2,1,0:T(8,128)(2,1)} %broadcast_in_dim.41), calls=%async_computation.5 | async-start | bytes 4718592 | tf_op jit(solution)/shard_map/all_to_all | solution.py:14
  391.6 2.5 copy-start.2
  406.6 36.9 %all-to-all-start.8 = ((bf16[32,8,2304]{2,1,0:T(8,128)(2,1)}), bf16[32,8,2304]{2,1,0:T(8,128)(2,1)}, u32[]{:S(2)}, u32[]{:S(2)}) async-start(bf16[32,8,2304]{2,1,0:T(8,128)(2,1)} %reduce_sum.135), calls=%async_computation.8 | async-start | bytes 2359296 | tf_op jit(solution)/shard_map/all_to_all | solution.py:55
  444.9 0.6 copy-start.4
  464.0 22.1 %all-to-all-start.11 = ((bf16[32,8,2304]{2,1,0:T(8,128)(2,1)}), bf16[32,8,2304]{2,1,0:T(8,128)(2,1)}, u32[]{:S(2)}, u32[]{:S(2)}) async-start(bf16[32,8,2304]{2,1,0:T(8,128)(2,1)} %broadcast_in_dim.44), calls=%async_computation.11 | async-start | bytes 2359296 | tf_op jit(solution)/shard_map/all_to_all | solution.py:14
  493.3 1.8 copy-start.1
  500.0 5.4 copy-start
  500.0 33.7 %all-to-all-start.13 = ((bf16[2,512,1152]{2,1,0:T(8,128)(2,1)}), bf16[2,512,1152]{2,1,0:T(8,128)(2,1)}, u32[]{:S(2)}, u32[]{:S(2)}) async-start(bf16[2,512,1152]{2,1,0:T(8,128)(2,1)} %broadcast_in_dim.46), calls=%async_computation.13 | async-start | bytes 4718592 | tf_op jit(solution)/shard_map/all_to_all | solution.py:14
  507.2 28.9 %copy-start.3 = (bf16[1,2,288,2304]{3,2,1,0:T(8,128)(2,1)S(1)}, bf16[1,2,288,2304]{3,2,1,0:T(8,128)(2,1)}, u32[]{:S(2)}) copy-start(bf16[1,2,288,2304]{3,2,1,0:T(8,128)(2,1)} %copy.52) | copy-start | bytes 7962628
  544.8 30.9 %copy-start.5 = (bf16[8,2304]{1,0:T(8,128)(2,1)S(1)}, bf16[8,2304]{1,0:T(8,128)(2,1)}, u32[]{:S(2)}) copy-start(bf16[8,2304]{1,0:T(8,128)(2,1)} %get-tuple-element.10) | copy-start | bytes 110596
where the time goes:
time: 586 us; the launch traced here: 577 us
  waiting for transfers between devices  220 us (38%)
  local copies, waits for them, and re-layouts  175 us (30%)
  starting transfers between devices  78.3 us (13%)
  blocking collectives  66.3 us (11%)
  other arithmetic  21.2 us (4%)
  matrix products  15.6 us (3%)
    all_to_all x1, waiting for transfers between devices, on_device(): lax.all_to_all(up_split, COL, split_axis=3, concat_axis=1, tiled=True)  69.1 us
    all_to_all x1, waiting for transfers between devices, on_device(): lax.all_to_all(gate_split, COL, split_axis=3, concat_axis=1, tiled=True)  62.8 us
    all_to_all x5, waiting for transfers between devices, sent_to_all(): return lax.all_to_all(copies, axis, split_axis=0, concat_axis=0, tiled=True)  35.2 us
    all_to_all x1, waiting for transfers between devices, on_device(): lax.all_to_all(down_weight, 'row', split_axis=2, concat_axis=1, tiled=True)  33.6 us
    all_to_all x1, local copies, waits for them, and re-layouts, on_device(): lax.all_to_all(down_weight, 'row', split_axis=2, concat_axis=1, tiled=True)  33 us
    all_to_all x5, blocking collectives, sent_to_all(): return lax.all_to_all(copies, axis, split_axis=0, concat_axis=0, tiled=True)  29.7 us
    all_to_all x5, starting transfers between devices, sent_to_all(): return lax.all_to_all(copies, axis, split_axis=0, concat_axis=0, tiled=True)  28.9 us
    reshape x2, local copies, waits for them, and re-layouts, on_device(): up_weight.reshape(layer_count, stored_rows, row_count, col_count, block_w...  25.9 us
  transfers between devices with their start and end apart: 9, of which 7 were waited for; matrix products, arithmetic and copies ran while one was open for 30% of the time, Pallas kernels for 0%

commit v1 on v0

--- a/solution.py
+++ b/solution.py
@@ -82,7 +82,12 @@
     )
     gate_tiles = gate_tiles.reshape(layer_count, tile_rows, tile_columns)
     up_tiles = up_tiles.reshape(layer_count, tile_rows, tile_columns)
-    down_tiles = lax.all_to_all(down_weight, "row", split_axis=2, concat_axis=1, tiled=True)
+    down_tiles = jnp.concatenate(
+        lax.all_to_all(
+            jnp.stack(jnp.split(down_weight, lax.axis_size("row"), axis=2)), "row", 0, 0
+        ),
+        axis=1,
+    )
     current = tokens
     for layer_index in range(layer_count):
         gate_up = jnp.concatenate((gate_tiles[layer_index], up_tiles[layer_index]), axis=1)

time: 586 us -> 547 us (0.933)
  local copies, waits for them, and re-layouts: 175 us -> 121 us
  blocking collectives: 66.3 us -> 97.1 us
  waiting for transfers between devices: 220 us -> 209 us
    all_to_all x1 -> x0, local copies, waits for them, and re-layouts: 33 us -> none  [on_device(): lax.all_to_all(down_weight, 'row', split_axis=2, concat_axis=1, tiled=True)]
    all_to_all x5 -> x6, blocking collectives: 29.7 us -> 60.5 us  [sent_to_all(): return lax.all_to_all(copies, axis, split_axis=0, concat_axis=0, tiled=True)]
    all_to_all x1, waiting for transfers between devices: 33.6 us -> 14.6 us  [on_device(): lax.all_to_all(jnp.stack(jnp.split(down_weight, lax.axis_size('row'), axi...]
    unnamed x13 -> x10, local copies, waits for them, and re-layouts: 20.3 us -> 3.63 us
    all_to_all x1, waiting for transfers between devices: 69.1 us -> 81.4 us  [on_device(): lax.all_to_all(up_split, COL, split_axis=3, concat_axis=1, tiled=True)]
    all_to_all x5 -> x4, starting transfers between devices: 28.9 us -> 23.7 us  [sent_to_all(): return lax.all_to_all(copies, axis, split_axis=0, concat_axis=0, tiled=True)]
    all_to_all x5 -> x4, waiting for transfers between devices: 35.2 us -> 30.5 us  [sent_to_all(): return lax.all_to_all(copies, axis, split_axis=0, concat_axis=0, tiled=True)]
  transfers between devices with their start and end apart: 9 -> 8, of which waited for: 7 -> 7; matrix products, arithmetic and copies ran while one was open for 30% -> 23% of each run, Pallas kernels for 0% -> 0%
where the time goes in v1:
time: 547 us; the launch traced here: 538 us
  waiting for transfers between devices  209 us (38%)
  local copies, waits for them, and re-layouts  121 us (22%)
  blocking collectives  97.1 us (18%)
  starting transfers between devices  73 us (13%)
  other arithmetic  21.9 us (4%)
  matrix products  15.6 us (3%)
    all_to_all x1, waiting for transfers between devices, on_device(): lax.all_to_all(up_split, COL, split_axis=3, concat_axis=1, tiled=True)  81.4 us
    all_to_all x1, waiting for transfers between devices, on_device(): lax.all_to_all(gate_split, COL, split_axis=3, concat_axis=1, tiled=True)  62.8 us
    all_to_all x6, blocking collectives, sent_to_all(): return lax.all_to_all(copies, axis, split_axis=0, concat_axis=0, tiled=True)  60.5 us
    all_to_all x4, waiting for transfers between devices, sent_to_all(): return lax.all_to_all(copies, axis, split_axis=0, concat_axis=0, tiled=True)  30.5 us
    reshape x2, local copies, waits for them, and re-layouts, on_device(): up_weight.reshape(layer_count, stored_rows, row_count, col_count, block_w...  25.9 us
    reshape x2, local copies, waits for them, and re-layouts, on_device(): gate_weight.reshape(layer_count, stored_rows, row_count, col_count, block...  25.9 us
    all_to_all x1, blocking collectives, sum_by_axis(): lax.all_to_all(nearer.astype(jnp.bfloat16), far, split_axis=0, concat_axi...  24.4 us
    all_to_all x4, starting transfers between devices, sent_to_all(): return lax.all_to_all(copies, axis, split_axis=0, concat_axis=0, tiled=True)  23.7 us
  transfers between devices with their start and end apart: 8, of which 7 were waited for; matrix products, arithmetic and copies ran while one was open for 23% of the time, Pallas kernels for 0%

profile of v1, /device:TPU:0, one launch (start us, length us, event | category | flops | bytes accessed | tf_op | source)
XLA Modules:
  0.0 537.9 jit_solution(2821316158094079224)
XLA Ops:
  0.0 0.9 fusion.42
  0.9 0.6 broadcast_in_dim.38
  1.5 3.3 all-to-all-start
  4.8 1.4 add_reduce_fusion.1
  6.2 2.3 all-to-all-done
  8.5 0.8 fusion.44
  9.3 1.1 broadcast_in_dim.39
  10.5 10.6 %all-to-all-start.1 = ((bf16[32,8,2304]{2,1,0:T(8,128)(2,1)}), bf16[32,8,2304]{2,1,0:T(8,128)(2,1)S(1)}, u32[]{:S(2)}, u32[]{:S(2)}) async-start(bf16[32,8,2304]{2,1,0:T(8,128)(2,1)} %broadcast_in_dim.39), calls=%async_computation.1 | async-start | bytes 2359296 | tf_op jit(solution)/shard_map/all_to_all | solution.py:14
  21.1 14.4 %reshape.62 = bf16[2,36,2,64,288]{4,3,2,0,1:T(8,128)(2,1)} reshape(bf16[2,36,36864]{2,0,1:T(2,128)(2,1)} %param.9) | data formatting | bytes 10616832 | tf_op jit(solution)/shard_map/reshape | solution.py:77
  35.5 11.4 %copy.27 = bf16[2,36,2,64,288]{4,2,1,0,3:T(2,128)(2,1)} copy(bf16[2,36,2,64,288]{4,3,2,0,1:T(8,128)(2,1)} %reshape.62) | data formatting | bytes 10616832 | tf_op jit(solution)/shard_map/reshape | solution.py:77
  47.1 5.6 %all_to_all.109 = bf16[2,32,8,2304]{3,2,1,0:T(8,128)(2,1)S(1)} all-to-all(bf16[2,32,8,2304]{3,2,1,0:T(8,128)(2,1)S(1)} %broadcast_in_dim.40), channel_id=1, replica_groups=mesh['row'=2,'col_0'=4,'col_1'=4,'col_2'=2,'col_3'=2] {'col_3'}, dimensions={0} | all-to-all | bytes 4718592 | tf_op jit(solution)/shard_map/all_to_all | solution.py:14
  52.8 10.6 %all-to-all-start.3 = ((bf16[2,36,2,64,288]{4,2,1,0,3:T(2,128)(2,1)}), bf16[2,36,2,64,288]{4,2,1,0,3:T(2,128)(2,1)}, u32[]{:S(2)}, u32[]{:S(2)}) async-start(bf16[2,36,2,64,288]{4,2,1,0,3:T(2,128)(2,1)} %copy.27), calls=%async_computation.3 | async-start | bytes 14155776 | tf_op jit(solution)/shard_map/all_to_all | solution.py:80
  63.4 14.4 %reshape.63 = bf16[2,36,2,64,288]{4,3,2,0,1:T(8,128)(2,1)} reshape(bf16[2,36,36864]{2,0,1:T(2,128)(2,1)} %param.10) | data formatting | bytes 10616832 | tf_op jit(solution)/shard_map/reshape | solution.py:78
  77.8 11.5 %copy.28 = bf16[2,36,2,64,288]{4,2,1,0,3:T(2,128)(2,1)} copy(bf16[2,36,2,64,288]{4,3,2,0,1:T(8,128)(2,1)} %reshape.63) | data formatting | bytes 10616832 | tf_op jit(solution)/shard_map/reshape | solution.py:78
  89.3 62.8 %all-to-all-done.3 = bf16[2,36,2,64,288]{4,2,1,0,3:T(2,128)(2,1)} async-done(((bf16[2,36,2,64,288]{4,2,1,0,3:T(2,128)(2,1)}), bf16[2,36,2,64,288]{4,2,1,0,3:T(2,128)(2,1)}, u32[]{:S(2)}, u32[]{:S(2)}) %all-to-all-start.3) | async-done | bytes 5308448 | tf_op jit(solution)/shard_map/all_to_all | solution.py:80
  152.1 16.1 %all-to-all-start.4 = ((bf16[2,36,2,64,288]{4,2,1,0,3:T(2,128)(2,1)}), bf16[2,36,2,64,288]{4,2,1,0,3:T(2,128)(2,1)}, u32[]{:S(2)}, u32[]{:S(2)}) async-start(bf16[2,36,2,64,288]{4,2,1,0,3:T(2,128)(2,1)} %copy.28), calls=%async_computation.4 | async-start | bytes 14155776 | tf_op jit(solution)/shard_map/all_to_all | solution.py:81
  168.2 2.9 slice_bitcast_fusion.1
  171.1 2.8 pad_maximum_fusion
  173.9 1.5 copy.26
  175.4 81.4 %all-to-all-done.4 = bf16[2,36,2,64,288]{4,2,1,0,3:T(2,128)(2,1)} async-done(((bf16[2,36,2,64,288]{4,2,1,0,3:T(2,128)(2,1)}), bf16[2,36,2,64,288]{4,2,1,0,3:T(2,128)(2,1)}, u32[]{:S(2)}, u32[]{:S(2)}) %all-to-all-start.4) | async-done | bytes 5308448 | tf_op jit(solution)/shard_map/all_to_all | solution.py:81
  256.8 6.2 %all-to-all-start.6 = ((bf16[2,2,288,2304]{3,2,1,0:T(8,128)(2,1)}), bf16[2,2,288,2304]{3,2,1,0:T(8,128)(2,1)}, u32[]{:S(2)}, u32[]{:S(2)}) async-start(bf16[2,2,288,2304]{3,2,1,0:T(8,128)(2,1)} %pad_maximum_fusion), calls=%async_computation.6 | async-start | bytes 10616832 | tf_op jit(solution)/shard_map/all_to_all | solution.py:86
  263.1 9.8 %fusion.61 = (bf16[1,64,36,2,1,288]{5,3,2,0,1,4:T(2,128)(2,1)S(1)}, bf16[1,64,36,2,1,288]{5,3,2,0,1,4:T(2,128)(2,1)}) fusion(bf16[2,64,36,2,1,288]{5,3,2,0,1,4:T(2,128)(2,1)} %bitcast.4), kind=kLoop, calls=%fused_computation.83 | loop fusion | bytes 10616832 | tf_op jit(solution)/shard_map/slice | solution.py:93
  272.9 8.4 %squeeze.22 = bf16[2304,576]{1,0:T(8,128)(2,1)} reshape(bf16[1,64,36,2,1,288]{5,3,2,0,1,4:T(2,128)(2,1)} %get-tuple-element.12) | data formatting | bytes 5308416 | tf_op jit(solution)/shard_map/squeeze | solution.py:93
  281.3 10.9 %fusion.62 = (bf16[1,64,36,2,1,288]{5,3,2,0,1,4:T(2,128)(2,1)}, bf16[1,64,36,2,1,288]{5,3,2,0,1,4:T(2,128)(2,1)}) fusion(bf16[2,64,36,2,1,288]{5,3,2,0,1,4:T(2,128)(2,1)} %bitcast.6), kind=kLoop, calls=%fused_computation.84 | loop fusion | bytes 10616832 | tf_op jit(solution)/shard_map/slice | solution.py:93
  292.2 8.0 %squeeze.23 = bf16[2304,576]{1,0:T(8,128)(2,1)} reshape(bf16[1,64,36,2,1,288]{5,3,2,0,1,4:T(2,128)(2,1)} %get-tuple-element.14) | data formatting | bytes 5308416 | tf_op jit(solution)/shard_map/squeeze | solution.py:93
  300.1 7.7 %fusion.11 = bf16[512,1152]{1,0:T(8,128)(2,1)} fusion(bf16[512,2304]{1,0:T(8,128)(2,1)} %bitcast.51, bf16[2304,576]{1,0:T(8,128)(2,1)} %squeeze.23, bf16[2304,576]{1,0:T(8,128)(2,1)} %squeeze.22), kind=kOutput, calls=%fused_computation.14 | convolution fusion | flops 2729115648 | bytes 8847360 | tf_op jit(solution)/shard_map/dot_general | solution.py:100
  307.8 14.6 %all-to-all-done.6 = bf16[2,2,288,2304]{3,2,1,0:T(8,128)(2,1)} async-done(((bf16[2,2,288,2304]{3,2,1,0:T(8,128)(2,1)}), bf16[2,2,288,2304]{3,2,1,0:T(8,128)(2,1)}, u32[]{:S(2)}, u32[]{:S(2)}) %all-to-all-start.6) | async-done | bytes 5308448 | tf_op jit(solution)/shard_map/all_to_all | solution.py:86
  322.4 2.9 broadcast_in_dim.41
  325.3 5.1 all-to-all-start.5
  330.4 5.3 fusion.63
  335.7 21.6 %all-to-all-done.5 = bf16[2,512,1152]{2,1,0:T(8,128)(2,1)} async-done(((bf16[2,512,1152]{2,1,0:T(8,128)(2,1)}), bf16[2,512,1152]{2,1,0:T(8,128)(2,1)}, u32[]{:S(2)}, u32[]{:S(2)}) %all-to-all-start.5) | async-done | bytes 2359328 | tf_op jit(solution)/shard_map/all_to_all | solution.py:14
  357.3 2.5 convert_reduce_fusion.1
  359.8 2.3 convolution_convert_fusion.1
  362.3 6.5 %all_to_all.110 = bf16[2,32,8,2304]{3,2,1,0:T(8,128)(2,1)} all-to-all(bf16[2,32,8,2304]{3,2,1,0:T(8,128)(2,1)S(1)} %bitcast.47), channel_id=1, replica_groups=mesh['row'=2,'col_0'=4,'col_1'=4,'col_2'=2,'col_3'=2] {'col_3'}, dimensions={0} | all-to-all | bytes 4718592 | tf_op jit(solution)/shard_map/all_to_all | solution.py:47
  368.8 3.4 reduce_sum.135
  372.2 16.3 %all-to-all-start.8 = ((bf16[32,8,2304]{2,1,0:T(8,128)(2,1)}), bf16[32,8,2304]{2,1,0:T(8,128)(2,1)}, u32[]{:S(2)}, u32[]{:S(2)}) async-start(bf16[32,8,2304]{2,1,0:T(8,128)(2,1)} %reduce_sum.135), calls=%async_computation.8 | async-start | bytes 2359296 | tf_op jit(solution)/shard_map/all_to_all | solution.py:55
  388.6 1.5 add_reduce_fusion
  390.0 19.6 %all-to-all-done.8 = bf16[32,8,2304]{2,1,0:T(8,128)(2,1)} async-done(((bf16[32,8,2304]{2,1,0:T(8,128)(2,1)}), bf16[32,8,2304]{2,1,0:T(8,128)(2,1)}, u32[]{:S(2)}, u32[]{:S(2)}) %all-to-all-start.8) | async-done | bytes 1179680 | tf_op jit(solution)/shard_map/all_to_all | solution.py:55
  409.6 1.4 convert_reduce_fusion.3
  411.1 0.6 copy-done.3
  411.8 6.1 %all_to_all.111 = f32[2,1,8]{2,1,0:T(1,128)S(1)} all-to-all(f32[2,1,8]{2,1,0:T(1,128)S(1)} %broadcast_in_dim.42), channel_id=1, replica_groups=mesh['row'=2,'col_0'=4,'col_1'=4,'col_2'=2,'col_3'=2] {'row'}, dimensions={0} | all-to-all | bytes 128 | tf_op jit(solution)/shard_map/all_to_all | solution.py:14
  417.9 0.5 reduce_sum.138
  418.5 0.7 add_rsqrt_fusion.2
  419.1 1.7 fusion.46
  420.8 6.1 %all_to_all.112 = f32[2,1,8]{2,1,0:T(1,128)S(1)} all-to-all(f32[2,1,8]{2,1,0:T(1,128)S(1)} %broadcast_in_dim.43), channel_id=1, replica_groups=mesh['row'=2,'col_0'=4,'col_1'=4,'col_2'=2,'col_3'=2] {'row'}, dimensions={0} | all-to-all | bytes 128 | tf_op jit(solution)/shard_map/all_to_all | solution.py:14
  427.4 0.6 add_rsqrt_fusion.1
  428.0 0.9 fusion.48
  428.9 1.1 broadcast_in_dim.44
  430.0 4.7 all-to-all-start.11
  434.7 4.0 squeeze.25
  438.7 6.9 %squeeze.26 = bf16[2304,576]{1,0:T(8,128)(2,1)S(1)} reshape(bf16[1,64,36,2,1,288]{5,3,2,0,1,4:T(2,128)(2,1)} %get-tuple-element.13) | data formatting | bytes 5308416 | tf_op jit(solution)/shard_map/squeeze | solution.py:93
  445.6 6.6 %all-to-all-done.11 = bf16[32,8,2304]{2,1,0:T(8,128)(2,1)} async-done(((bf16[32,8,2304]{2,1,0:T(8,128)(2,1)}), bf16[32,8,2304]{2,1,0:T(8,128)(2,1)}, u32[]{:S(2)}, u32[]{:S(2)}) %all-to-all-start.11) | async-done | bytes 1179680 | tf_op jit(solution)/shard_map/all_to_all | solution.py:14
  452.3 1.4 broadcast_in_dim.45
  453.7 5.6 %all_to_all.113 = bf16[2,32,8,2304]{3,2,1,0:T(8,128)(2,1)S(1)} all-to-all(bf16[2,32,8,2304]{3,2,1,0:T(8,128)(2,1)S(1)} %broadcast_in_dim.45), channel_id=1, replica_groups=mesh['row'=2,'col_0'=4,'col_1'=4,'col_2'=2,'col_3'=2] {'col_3'}, dimensions={0} | all-to-all | bytes 4718592 | tf_op jit(solution)/shard_map/all_to_all | solution.py:14
  459.5 1.7 copy-done
  461.1 3.2 fusion.8
  464.6 31.0 %all_to_all.114 = bf16[2,512,1152]{2,1,0:T(8,128)(2,1)S(1)} all-to-all(bf16[2,512,1152]{2,1,0:T(8,128)(2,1)S(1)} %broadcast_in_dim.46), channel_id=1, replica_groups=mesh['row'=2,'col_0'=4,'col_1'=4,'col_2'=2,'col_3'=2] {'row'}, dimensions={0} | all-to-all | bytes 4718592 | tf_op jit(solution)/shard_map/all_to_all | solution.py:14
  496.0 1.3 copy-done.1
  497.3 2.3 convolution_convert_fusion
  499.8 5.6 %all_to_all.115 = bf16[2,32,8,2304]{3,2,1,0:T(8,128)(2,1)S(1)} all-to-all(bf16[2,32,8,2304]{3,2,1,0:T(8,128)(2,1)S(1)} %bitcast.48), channel_id=1, replica_groups=mesh['row'=2,'col_0'=4,'col_1'=4,'col_2'=2,'col_3'=2] {'col_3'}, dimensions={0} | all-to-all | bytes 4718592 | tf_op jit(solution)/shard_map/all_to_all | solution.py:47
  505.4 0.6 reduce_sum.142
  506.1 24.4 %all_to_all.116 = bf16[32,8,2304]{2,1,0:T(8,128)(2,1)S(1)} all-to-all(bf16[32,8,2304]{2,1,0:T(8,128)(2,1)S(1)} %reduce_sum.142), channel_id=1, replica_groups=mesh['row'=2,'col_0'=4,'col_1'=4,'col_2'=2,'col_3'=2] {'col_0','col_1','..., dimensions={0} | all-to-all | bytes 2359296 | tf_op jit(solution)/shard_map/all_to_all | solution.py:55
  530.8 6.1 %all_to_all.117 = f32[2,1,8]{2,1,0:T(1,128)S(1)} all-to-all(f32[2,1,8]{2,1,0:T(1,128)S(1)} %broadcast_in_dim.47), channel_id=1, replica_groups=mesh['row'=2,'col_0'=4,'col_1'=4,'col_2'=2,'col_3'=2] {'row'}, dimensions={0} | all-to-all | bytes 128 | tf_op jit(solution)/shard_map/all_to_all | solution.py:14
  537.0 0.7 fusion.49
  (25 shorter events, 2.2 us)
Async XLA Ops:
  1.5 7.0 %all-to-all-start = ((f32[2,1,8]{2,1,0:T(1,128)}), f32[2,1,8]{2,1,0:T(1,128)S(1)}, u32[]{:S(2)}, u32[]{:S(2)}) async-start(f32[2,1,8]{2,1,0:T(1,128)} %broadcast_in_dim.38), calls=%async_computation | async-start | bytes 2048 | tf_op jit(solution)/shard_map/all_to_all | solution.py:14
  10.5 36.5 %all-to-all-start.1 = ((bf16[32,8,2304]{2,1,0:T(8,128)(2,1)}), bf16[32,8,2304]{2,1,0:T(8,128)(2,1)S(1)}, u32[]{:S(2)}, u32[]{:S(2)}) async-start(bf16[32,8,2304]{2,1,0:T(8,128)(2,1)} %broadcast_in_dim.39), calls=%async_computation.1 | async-start | bytes 2359296 | tf_op jit(solution)/shard_map/all_to_all | solution.py:14
  52.8 99.3 %all-to-all-start.3 = ((bf16[2,36,2,64,288]{4,2,1,0,3:T(2,128)(2,1)}), bf16[2,36,2,64,288]{4,2,1,0,3:T(2,128)(2,1)}, u32[]{:S(2)}, u32[]{:S(2)}) async-start(bf16[2,36,2,64,288]{4,2,1,0,3:T(2,128)(2,1)} %copy.27), calls=%async_computation.3 | async-start | bytes 14155776 | tf_op jit(solution)/shard_map/all_to_all | solution.py:80
  152.1 104.7 %all-to-all-start.4 = ((bf16[2,36,2,64,288]{4,2,1,0,3:T(2,128)(2,1)}), bf16[2,36,2,64,288]{4,2,1,0,3:T(2,128)(2,1)}, u32[]{:S(2)}, u32[]{:S(2)}) async-start(bf16[2,36,2,64,288]{4,2,1,0,3:T(2,128)(2,1)} %copy.28), calls=%async_computation.4 | async-start | bytes 14155776 | tf_op jit(solution)/shard_map/all_to_all | solution.py:81
  256.8 65.6 %all-to-all-start.6 = ((bf16[2,2,288,2304]{3,2,1,0:T(8,128)(2,1)}), bf16[2,2,288,2304]{3,2,1,0:T(8,128)(2,1)}, u32[]{:S(2)}, u32[]{:S(2)}) async-start(bf16[2,2,288,2304]{3,2,1,0:T(8,128)(2,1)} %pad_maximum_fusion), calls=%async_computation.6 | async-start | bytes 10616832 | tf_op jit(solution)/shard_map/all_to_all | solution.py:86
  325.3 32.0 %all-to-all-start.5 = ((bf16[2,512,1152]{2,1,0:T(8,128)(2,1)}), bf16[2,512,1152]{2,1,0:T(8,128)(2,1)}, u32[]{:S(2)}, u32[]{:S(2)}) async-start(bf16[2,512,1152]{2,1,0:T(8,128)(2,1)} %broadcast_in_dim.41), calls=%async_computation.5 | async-start | bytes 4718592 | tf_op jit(solution)/shard_map/all_to_all | solution.py:14
  357.3 2.5 copy-start.2
  372.2 37.4 %all-to-all-start.8 = ((bf16[32,8,2304]{2,1,0:T(8,128)(2,1)}), bf16[32,8,2304]{2,1,0:T(8,128)(2,1)}, u32[]{:S(2)}, u32[]{:S(2)}) async-start(bf16[32,8,2304]{2,1,0:T(8,128)(2,1)} %reduce_sum.135), calls=%async_computation.8 | async-start | bytes 2359296 | tf_op jit(solution)/shard_map/all_to_all | solution.py:55
  411.1 0.6 copy-start.3
  430.0 22.3 %all-to-all-start.11 = ((bf16[32,8,2304]{2,1,0:T(8,128)(2,1)}), bf16[32,8,2304]{2,1,0:T(8,128)(2,1)}, u32[]{:S(2)}, u32[]{:S(2)}) async-start(bf16[32,8,2304]{2,1,0:T(8,128)(2,1)} %broadcast_in_dim.44), calls=%async_computation.11 | async-start | bytes 2359296 | tf_op jit(solution)/shard_map/all_to_all | solution.py:14
  459.3 1.8 copy-start
  495.6 1.8 copy-start.1
  506.1 30.9 %copy-start.4 = (bf16[8,2304]{1,0:T(8,128)(2,1)S(1)}, bf16[8,2304]{1,0:T(8,128)(2,1)}, u32[]{:S(2)}) copy-start(bf16[8,2304]{1,0:T(8,128)(2,1)} %get-tuple-element.10) | copy-start | bytes 110596
